TPU v7x, 32 devices: a whole 2x2x4 slice. The times are simulated.
32 devices in a mesh: seq: 2 (over core), batch: 16 (over z, y, x).
Axes of the slice: x: 2, y: 2, z: 4, core: 2. Of those that a mesh axis runs over, the one named last changes fastest.
Arguments:
- queries: bfloat16 [16, 1024, 1024], P('batch', 'seq'), may hold values from -6 to 6
- keys: bfloat16 [16, 1024, 1024], P('batch', 'seq'), may hold values from -6 to 6
- values: bfloat16 [16, 1024, 2048], P('batch', 'seq'), may hold values from -6 to 6
- gate_rate: bfloat16 [16, 1024, 1024], P('batch', 'seq'), may hold values from 0.5 to 2
- segment_ids: int32 [16, 1024], P('batch', 'seq'), may hold values from 0 to 2, never falling along the last dimension, each value on 1 to 512 neighbouring positions
- decay_exps: int32 [4], replicated, may hold values from 0 to 13
- out_weight: bfloat16 [2048, 2048], P('batch'), may hold values from -0.125 to 0.125
Outputs:
- projected: bfloat16 [16, 1024, 2048], P('batch', 'seq')
Inputs may be any that keep to these rules, and one draw needn't show every extreme that they name: `segment_ids`: within each stream the ids never fall and start at 0; each of the 3 ids covers 1 to 512 consecutive tokens, one of them exactly 512.
All inputs are finite; a program needn't handle non-finite values.
Results may differ from a plain program's by a relative error of at most 0.004.
The roundings to bfloat16 on the way count: a program that leaves them out, or rounds other values in their place, can miss the bound.
Values may be sent and summed in bfloat16 or wider, within the bound.
A program may use at most 128 MiB of HBM per device.

v0:
```python
import functools
import math

import jax
import jax.numpy as jnp
from jax import lax
from jax.experimental import pallas as pl
from jax.experimental.pallas import tpu as pltpu
from jax.sharding import PartitionSpec as P

MESH = pl.DeviceIdType.MESH
CHUNK = 256
TILE = 512


def chip_grid(mesh):
    count = mesh.shape["batch"]
    try:
        axis = mesh.axis_names.index("batch")
        line = mesh.devices.swapaxes(0, axis).reshape(count, -1)[:, 0]
        coords = [tuple(device.coords) for device in line]
        sizes = [len({c[i] for c in coords}) for i in (2, 1, 0)]
        lows = [min(c[i] for c in coords) for i in (2, 1, 0)]
        for index, c in enumerate(coords):
            z, y, x = (c[2] - lows[0], c[1] - lows[1], c[0] - lows[2])
            if (z * sizes[1] + y) * sizes[2] + x != index:
                return (count, 1, 1)
        return tuple(sizes)
    except Exception:
        return (count, 1, 1)


def split(x):
    high = x.astype(jnp.bfloat16)
    return high, (x - high.astype(jnp.float32)).astype(jnp.bfloat16)


def mm(a, b):
    return lax.dot_general(a, b, (((1,), (0,)), ((), ())), preferred_element_type=jnp.float32)


def mm_t(a, b):
    return lax.dot_general(a, b, (((1,), (1,)), ((), ())), preferred_element_type=jnp.float32)


def t_mm(a, b):
    return lax.dot_general(a, b, (((0,), (0,)), ((), ())), preferred_element_type=jnp.float32)


def kernel(
    grid, peers, heads, chunk,
    q_hbm, k_hbm, v_hbm, g_hbm, seg_ref, exps_ref, w_hbm,
    out_ref,
    q_ref, k_ref, v_ref, g_ref, w_ref, hidden, acc, seg_in, state_in, state_out,
    load_sem, seg_sem, state_send, state_recv, send_sem, recv_sem, climb_sem, msend, mrecv,
):
    Z, Y, X = grid
    s = lax.axis_index("seq")
    me = lax.axis_index("batch")
    length, keys = q_ref.shape
    key_width = keys // heads
    value_width = v_ref.shape[1] // heads
    rows = w_hbm.shape[0]
    columns = w_ref.shape[1]
    part = columns // peers
    plane_rows = rows * X * Y
    a = me // (X * Y)
    swap = X == Y
    nb, nc = X, Y

    def strides(core):
        if not swap:
            return 1, X
        even = lax.rem(core, 2) == 0
        return jnp.where(even, 1, X), jnp.where(even, X, 1)

    def chip_at(core, plane, db, dc):
        sb, sc = strides(core)
        b = lax.rem(me // sb, nb)
        c = lax.rem(me // sc, nc)
        return (
            plane * (X * Y)
            + lax.rem(b - db + nb, nb) * sb
            + lax.rem(c - dc + nc, nc) * sc
        )

    near = jnp.minimum(a, Z - 1 - a)

    def plane_at(g):
        side = jnp.where(lax.rem(g, 2) == 1, -1, 1)
        rest = jnp.where(a < Z - 1 - a, g, Z - 1 - g)
        return jnp.where(g <= 2 * near, a + (g + 1) // 2 * side, rest)

    def label(plane, db, dc):
        return (plane * nb + db) * nc + dc

    def block(core, chip):
        return w_ref.at[
            pl.ds(pl.multiple_of(chip * rows, rows), rows),
            pl.ds(pl.multiple_of(core * part, part), part),
        ]

    def relay(held, step):
        here = block(s, chip_at(s, *held))
        target = chip_at(s, a, -step[0], -step[1])
        index = label(held[0], held[1] + step[0], held[2] + step[1])
        return pltpu.make_async_remote_copy(
            src_ref=here, dst_ref=here, send_sem=send_sem.at[index], recv_sem=recv_sem.at[index],
            device_id={"batch": target}, device_id_type=MESH,
        )

    def climb(plane, way):
        here = block(s, chip_at(s, plane, 0, 0))
        target = me + (X * Y if way else -X * Y)
        return pltpu.make_async_remote_copy(
            src_ref=here, dst_ref=here, send_sem=climb_sem.at[way, plane],
            recv_sem=recv_sem.at[label(plane, 0, 0)],
            device_id={"batch": target}, device_id_type=MESH,
        )

    def arrival(plane, db, dc):
        here = block(s, chip_at(s, plane, db, dc))
        index = label(plane, db, dc)
        other = lax.rem(me + 1, X * Y * Z)
        return pltpu.make_async_remote_copy(
            src_ref=here, dst_ref=here, send_sem=send_sem.at[index], recv_sem=recv_sem.at[index],
            device_id={"batch": other}, device_id_type=MESH,
        )

    def mirror(plane, db, dc, ds, core):
        here = block(core, chip_at(core, plane, db, dc))
        index = label(plane, db, dc)
        return pltpu.make_async_remote_copy(
            src_ref=here, dst_ref=here,
            send_sem=msend.at[ds - 1, index], recv_sem=mrecv.at[ds - 1, index],
            device_id={"seq": lax.rem(s + ds, peers)}, device_id_type=MESH,
        )

    def share(plane, db, dc):
        for ds in range(1, peers):
            mirror(plane, db, dc, ds, s).start()

    def forward_plane(plane):
        for db in range(1, nb):
            relay((plane, 0, 0), (db, 0)).start()
        for dc in range(1, nc):
            relay((plane, 0, 0), (0, dc)).start()

    def middle(g):
        @pl.when(g < Z)
        def _():
            plane = plane_at(g)
            for db in range(1, nb):
                arrival(plane, db, 0).wait_recv()
                for dc in range(1, nc):
                    relay((plane, db, 0), (0, dc)).start()
                share(plane, db, 0)

    def enter(g):
        @pl.when(g < Z)
        def _():
            plane = plane_at(g)
            arrival(plane, 0, 0).wait_recv()

            @pl.when(jnp.logical_and(plane < a, a < Z - 1))
            def _():
                climb(plane, 1).start()

            @pl.when(jnp.logical_and(plane > a, a > 0))
            def _():
                climb(plane, 0).start()

            forward_plane(plane)
            share(plane, 0, 0)

    def tail(g):
        @pl.when(g < Z)
        def _():
            plane = plane_at(g)
            for dc in range(1, nc):
                for db in range(nb):
                    arrival(plane, db, dc).wait_recv()
                    share(plane, db, dc)

    def mirrored(g):
        plane = plane_at(g)
        for ds in range(1, peers):
            core = lax.rem(s - ds + peers, peers)
            for db in range(nb):
                for dc in range(nc):
                    def wait():
                        mirror(plane, db, dc, ds, core).wait_recv()
                    if db or dc:
                        wait()
                    else:
                        pl.when(g > 0)(wait)

    loads = [
        pltpu.make_async_copy(
            w_hbm, w_ref.at[pl.ds(pl.multiple_of(me * rows, rows), rows), :], load_sem.at[0]
        ),
        pltpu.make_async_copy(g_hbm, g_ref, load_sem.at[1]),
        pltpu.make_async_copy(k_hbm, k_ref, load_sem.at[2]),
        pltpu.make_async_copy(q_hbm, q_ref, load_sem.at[3]),
        pltpu.make_async_copy(v_hbm, v_ref, load_sem.at[4]),
    ]
    for load in loads:
        load.start()

    barrier = pltpu.get_barrier_semaphore()
    friends = [{"batch": chip_at(s, a, d, 0)} for d in range(1, nb)]
    friends += [{"batch": chip_at(s, a, 0, d)} for d in range(1, nc)]
    friends += [{"seq": lax.rem(s + d, peers)} for d in range(1, peers)]
    for friend in friends:
        pl.semaphore_signal(barrier, inc=1, device_id=friend, device_id_type=MESH)

    @pl.when(a < Z - 1)
    def _():
        pl.semaphore_signal(barrier, inc=1, device_id={"batch": me + X * Y}, device_id_type=MESH)

    @pl.when(a > 0)
    def _():
        pl.semaphore_signal(barrier, inc=1, device_id={"batch": me - X * Y}, device_id_type=MESH)

    above, below = jnp.where(a < Z - 1, 1, 0), jnp.where(a > 0, 1, 0)
    pl.semaphore_wait(barrier, len(friends) + above + below)

    loads[0].wait()

    @pl.when(a < Z - 1)
    def _():
        climb(a, 1).start()

    @pl.when(a > 0)
    def _():
        climb(a, 0).start()

    forward_plane(a)

    def next_core():
        return {"seq": lax.rem(s + 1, peers)}

    seg_copy = pltpu.make_async_remote_copy(
        src_ref=seg_ref, dst_ref=seg_in, send_sem=seg_sem.at[0], recv_sem=seg_sem.at[1],
        device_id=next_core(), device_id_type=MESH,
    )

    def state_copy(h):
        return pltpu.make_async_remote_copy(
            src_ref=state_out.at[h], dst_ref=state_in.at[h],
            send_sem=state_send.at[h], recv_sem=state_recv.at[h],
            device_id=next_core(), device_id_type=MESH,
        )

    @pl.when(s < peers - 1)
    def _():
        seg_copy.start()

    @pl.when(s == 0)
    def _():
        state_in[...] = jnp.zeros_like(state_in)
        seg_in[...] = jnp.full(seg_in.shape, -1, jnp.int32)

    for load in loads[1:]:
        load.wait()

    @pl.when(s > 0)
    def _():
        seg_copy.wait_recv()

    order_t = lax.broadcasted_iota(jnp.int32, (chunk, chunk), 0)
    order_s = lax.broadcasted_iota(jnp.int32, (chunk, chunk), 1)
    causal = order_t >= order_s
    triangle = jnp.where(causal, 1.0, 0.0).astype(jnp.bfloat16)
    seg_row = seg_ref[...].astype(jnp.float32)
    before = seg_in[...].astype(jnp.float32)[:, length - 1:]
    seg_wide = jnp.broadcast_to(seg_row, (128, length)).T

    def first():
        middle(0)
        enter(1)

    def second():
        enter(2)
        middle(1)

    def third():
        enter(3)
        tail(0)

    events = [first, second, third]
    early = min(len(events), heads - 1)

    def head(h, _):
        turn = h - jnp.where(s == 0, 1, 0)
        for number, event in enumerate(events[:early]):
            pl.when(turn == number)(event)

        exponent = jnp.full((1, key_width), exps_ref[h], jnp.int32).astype(jnp.float32)
        scale = jnp.exp2(-exponent) * (-1.0 / 16.0)

        @pl.when(s > 0)
        def _():
            state_copy(h).wait_recv()

        state = state_in[h]
        previous = before
        key_cols = pl.ds(pl.multiple_of(h * key_width, key_width), key_width)
        value_cols = pl.ds(pl.multiple_of(h * value_width, value_width), value_width)
        for i in range(length // chunk):
            now = pl.ds(i * chunk, chunk)
            log = mm(triangle, g_ref[now, key_cols]) * scale
            fall = jnp.exp(log)
            raised_q = q_ref[now, key_cols].astype(jnp.float32) * (fall * (1.0 / math.sqrt(key_width)))
            raised_k = k_ref[now, key_cols].astype(jnp.float32) * jnp.exp(-log)
            value = v_ref[now, value_cols]
            q_hi, q_lo = split(raised_q)
            k_hi, k_lo = split(raised_k)
            row = seg_row[:, i * chunk:(i + 1) * chunk]
            column = seg_wide[i * chunk:(i + 1) * chunk, :1]
            scores = mm_t(q_hi, k_hi) + mm_t(q_hi, k_lo) + mm_t(q_lo, k_hi)
            scores = jnp.where(jnp.logical_and(causal, column == row), scores, 0.0)
            p_hi, p_lo = split(scores)
            s_hi, s_lo = split(state)
            carried = mm_t(q_hi, s_hi) + mm_t(q_hi, s_lo) + mm_t(q_lo, s_hi)
            mixed = mm(p_hi, value) + mm(p_lo, value)
            mixed = mixed + jnp.where(column == previous, carried, 0.0)
            power = jnp.mean(mixed * mixed, axis=-1, keepdims=True)
            hidden[now, value_cols] = (mixed * lax.rsqrt(power + 1.0)).astype(jnp.bfloat16)
            final = fall[chunk - 1:, :]
            last = row[:, chunk - 1:]
            weighted = jnp.where(column == last, raised_k * final, 0.0)
            w_hi, w_lo = split(weighted)
            kept = jnp.where(last == previous, state * final, 0.0)
            state = kept + t_mm(value, w_hi) + t_mm(value, w_lo)
            previous = last

        @pl.when(s < peers - 1)
        def _():
            state_out[h] = state
            state_copy(h).start()

        return 0

    lax.fori_loop(0, heads, head, 0)
    for event in events[early:]:
        event()

    def plane_start(g):
        return pl.multiple_of(plane_at(g) * plane_rows, plane_rows)

    def project(g):
        start = plane_start(g)
        left = hidden[:, pl.ds(start, plane_rows)]
        for tile in range(columns // TILE):
            cols = pl.ds(tile * TILE, TILE)
            product = mm(left, w_ref[pl.ds(start, plane_rows), cols])

            @pl.when(g == 0)
            def _():
                acc[:, cols] = product

            @pl.when(g > 0)
            def _():
                acc[:, cols] += product

    def step(g, _):
        middle(g + 2)
        enter(g + 4)
        mirrored(g)
        project(g)
        tail(g + 1)
        return 0

    lax.fori_loop(0, Z - 1, step, 0)
    mirrored(Z - 1)
    start = plane_start(Z - 1)
    left = hidden[:, pl.ds(start, plane_rows)]
    for tile in range(columns // TILE):
        cols = pl.ds(tile * TILE, TILE)
        product = mm(left, w_ref[pl.ds(start, plane_rows), cols])
        total = acc[:, cols] + product if Z > 1 else product
        out_ref[:, cols] = total.astype(jnp.bfloat16)

    @pl.when(s < peers - 1)
    def _():
        seg_copy.wait_send()

        def sent(h, _):
            state_copy(h).wait_send()
            return 0

        lax.fori_loop(0, heads, sent, 0)

    def sent_plane(plane, _):
        for db in range(nb):
            for dc in range(nc):
                if db or dc:
                    arrival(plane, db, dc).wait_send()

                def wait():
                    for ds in range(1, peers):
                        mirror(plane, db, dc, ds, s).wait_send()

                if db or dc:
                    wait()
                else:
                    pl.when(plane != a)(wait)

        @pl.when(jnp.logical_and(plane <= a, a < Z - 1))
        def _():
            climb(plane, 1).wait_send()

        @pl.when(jnp.logical_and(plane >= a, a > 0))
        def _():
            climb(plane, 0).wait_send()

        return 0

    lax.fori_loop(0, Z, sent_plane, 0)


def local(grid, peers, queries, keys, values, gate_rate, segment_ids, decay_exps, out_weight):
    groups, length, key_features = queries.shape
    heads = decay_exps.shape[0]
    features = values.shape[2]
    columns = out_weight.shape[1]
    chips = grid[0] * grid[1] * grid[2]
    chunk = min(CHUNK, length)
    kw, vw = key_features // heads, features // heads
    bf16, f32 = jnp.bfloat16, jnp.float32
    anywhere = pl.BlockSpec(memory_space=pl.ANY)
    call = pl.pallas_call(
        functools.partial(kernel, grid, peers, heads, chunk),
        out_shape=pltpu.VMEM((length, columns), bf16),
        in_specs=[anywhere] * 4
        + [pl.BlockSpec(memory_space=pltpu.VMEM), pl.BlockSpec(memory_space=pltpu.SMEM), anywhere],
        out_specs=pl.BlockSpec(memory_space=pltpu.VMEM),
        scratch_shapes=[
            pltpu.VMEM((length, key_features), bf16),
            pltpu.VMEM((length, key_features), bf16),
            pltpu.VMEM((length, features), bf16),
            pltpu.VMEM((length, key_features), bf16),
            pltpu.VMEM((features, columns), bf16),
            pltpu.VMEM((length, features), bf16),
            pltpu.VMEM((length, columns), f32),
            pltpu.VMEM((1, length), jnp.int32),
            pltpu.VMEM((heads, vw, kw), f32),
            pltpu.VMEM((heads, vw, kw), f32),
            pltpu.SemaphoreType.DMA((5,)),
            pltpu.SemaphoreType.DMA((2,)),
            pltpu.SemaphoreType.DMA((heads,)),
            pltpu.SemaphoreType.DMA((heads,)),
            pltpu.SemaphoreType.DMA((chips,)),
            pltpu.SemaphoreType.DMA((chips,)),
            pltpu.SemaphoreType.DMA((2, grid[0])),
            pltpu.SemaphoreType.DMA((max(peers - 1, 1), chips)),
            pltpu.SemaphoreType.DMA((max(peers - 1, 1), chips)),
        ],
        compiler_params=pltpu.CompilerParams(
            collective_id=0, has_side_effects=True, vmem_limit_bytes=61 * 1024 * 1024
        ),
        name="gla_project",
    )
    outs = [
        call(queries[n], keys[n], values[n], gate_rate[n], segment_ids[n:n + 1], decay_exps, out_weight)
        for n in range(groups)
    ]
    return jnp.stack(outs)


def solution(mesh):
    in_specs = (
        P("batch", "seq", None),
        P("batch", "seq", None),
        P("batch", "seq", None),
        P("batch", "seq", None),
        P("batch", "seq"),
        P(),
        P("batch", None),
    )
    body = functools.partial(local, chip_grid(mesh), mesh.shape["seq"])
    return jax.shard_map(
        body, mesh=mesh, in_specs=in_specs, out_specs=P("batch", "seq", None), check_vma=False
    )
```

profile of v0, /device:TPU:0, one launch (start us, length us, event | category | flops | bytes accessed | tf_op | source)
XLA Modules:
  0.0 48.0 jit_solution(1965594679093055702)
XLA Ops:
  0.0 46.7 %gla_project.1 = bf16[512,2048]{1,0:T(8,128)(2,1)S(1)} custom-call(bf16[512,1024]{1,0:T(8,128)(2,1)} %bitcast.7, bf16[512,1024]{1,0:T(8,128)(2,1)} %bitcast.8, bf16[512,2048]{1,0:T(8,128)(2,1)} %bitcast.6, bf16[512,1024]{1,0:T(8,128)(2,1)} %bitcast.9, s32[1,512]{1,0:T(1,128)} %seg_ref.1, s32[4]{0:T(128)} %exps_ref.1, bf16[128,2048]{1,0:T(8,128)(2,1)} %w_hbm.1), custom_call_target="tpu_custom_call" | custom-call | tf_op jit(solution)/shard_map/gla_project/pallas_call | solution.py:466
  46.7 1.3 %copy.9 = bf16[1,512,2048]{2,1,0:T(8,128)(2,1)} copy(bf16[1,512,2048]{2,1,0:T(8,128)(2,1)S(1)} %bitcast.5) | data formatting | bytes 4194304
where the time goes:
time: 48.2 us; the launch traced here: 48 us
  Pallas kernels  46.7 us (97%)
  local copies, waits for them, and re-layouts  1.32 us (3%)
    pallas_call x1, Pallas kernels, local(): call(queries[n], keys[n], values[n], gate_rate[n], segment_ids[n:n + 1],...  46.7 us
    unnamed x1, local copies, waits for them, and re-layouts  1.32 us

commit v1 on v0

--- a/solution.py
+++ b/solution.py
@@ -11,6 +11,7 @@
 MESH = pl.DeviceIdType.MESH
 CHUNK = 256
 TILE = 512
+PIECES = 4
 
 
 def chip_grid(mesh):
@@ -47,12 +48,30 @@
     return lax.dot_general(a, b, (((0,), (0,)), ((), ())), preferred_element_type=jnp.float32)
 
 
+def thresholds(grid):
+    Z, Y, X = grid
+    beside, corner = X + Y - 2, (X - 1) * (Y - 1)
+    picked = []
+    for a in range(Z):
+        best = None
+        for reach in range(Z):
+            far = [g for g in range(Z) if abs(g - a) > reach]
+            below = a + corner * len([g for g in far if g < a])
+            above = Z - 1 - a + corner * len([g for g in far if g > a])
+            inside = (Z * beside + (Z - len(far)) * corner) / 2
+            load = max(below, above, inside)
+            if best is None or load < best[0]:
+                best = (load, reach)
+        picked.append(best[1])
+    return picked
+
+
 def kernel(
-    grid, peers, heads, chunk,
+    grid, peers, heads, chunk, pieces,
     q_hbm, k_hbm, v_hbm, g_hbm, seg_ref, exps_ref, w_hbm,
     out_ref,
     q_ref, k_ref, v_ref, g_ref, w_ref, hidden, acc, seg_in, state_in, state_out,
-    load_sem, seg_sem, state_send, state_recv, send_sem, recv_sem, climb_sem, msend, mrecv,
+    load_sem, seg_sem, state_send, state_recv, side_sem, relay_sem, climb_sem, corner_sem, recv_sem, msend, mrecv,
 ):
     Z, Y, X = grid
     s = lax.axis_index("seq")
@@ -61,12 +80,17 @@
     key_width = keys // heads
     value_width = v_ref.shape[1] // heads
     rows = w_hbm.shape[0]
+    depth = rows // pieces
     columns = w_ref.shape[1]
     part = columns // peers
     plane_rows = rows * X * Y
     a = me // (X * Y)
     swap = X == Y
     nb, nc = X, Y
+    sides = [(db, 0) for db in range(1, nb)]
+    fronts = [(0, dc) for dc in range(1, nc)]
+    corners = [(db, dc) for db in range(1, nb) for dc in range(1, nc)]
+    table = thresholds(grid)
 
     def strides(core):
         if not swap:
@@ -91,109 +115,180 @@
         rest = jnp.where(a < Z - 1 - a, g, Z - 1 - g)
         return jnp.where(g <= 2 * near, a + (g + 1) // 2 * side, rest)
 
+    def reach_of(plane):
+        reach = jnp.int32(table[0])
+        for index in range(1, Z):
+            reach = jnp.where(plane == index, table[index], reach)
+        return reach
+
+    reach = reach_of(a)
+    reach_by = {-1: reach_of(a - 1), 1: reach_of(a + 1)}
+    has = {-1: a > 0, 1: a < Z - 1}
+
     def label(plane, db, dc):
         return (plane * nb + db) * nc + dc
 
-    def block(core, chip):
+    def block(core, start, count):
         return w_ref.at[
-            pl.ds(pl.multiple_of(chip * rows, rows), rows),
+            pl.ds(pl.multiple_of(start, depth), count),
             pl.ds(pl.multiple_of(core * part, part), part),
         ]
 
-    def relay(held, step):
-        here = block(s, chip_at(s, *held))
-        target = chip_at(s, a, -step[0], -step[1])
-        index = label(held[0], held[1] + step[0], held[2] + step[1])
+    def send(held, to, sem, device, piece):
+        here = block(s, chip_at(s, *held) * rows + piece * depth, depth)
         return pltpu.make_async_remote_copy(
-            src_ref=here, dst_ref=here, send_sem=send_sem.at[index], recv_sem=recv_sem.at[index],
-            device_id={"batch": target}, device_id_type=MESH,
+            src_ref=here, dst_ref=here, send_sem=sem, recv_sem=recv_sem.at[label(*to) * pieces + piece],
+            device_id={"batch": device}, device_id_type=MESH,
         )
 
-    def climb(plane, way):
-        here = block(s, chip_at(s, plane, 0, 0))
-        target = me + (X * Y if way else -X * Y)
+    def sideways(plane, piece):
+        for db, _ in sides:
+            send((plane, 0, 0), (plane, db, 0), side_sem.at[0], chip_at(s, a, -db, 0), piece).start()
+
+    def forwards(plane, piece):
+        for _, dc in fronts:
+            send((plane, 0, 0), (plane, 0, dc), side_sem.at[1], chip_at(s, a, 0, -dc), piece).start()
+
+    def climb(plane, side, piece):
+        to = (plane, 0, 0)
+        send(to, to, climb_sem.at[(side + 1) // 2, plane], me + side * X * Y, piece).start()
+
+    def climb_corners(plane, side, piece):
+        for corner in corners:
+            to = (plane, *corner)
+            send(to, to, corner_sem.at[(side + 1) // 2, plane], me + side * X * Y, piece).start()
+
+    def wait_piece(plane, db, dc, piece):
+        to = (plane, db, dc)
+        send(to, to, side_sem.at[0], lax.rem(me + 1, X * Y * Z), piece).wait_recv()
+
+    def share(plane, db, dc, piece):
+        here = block(s, chip_at(s, plane, db, dc) * rows + piece * depth, depth)
+        for ds in range(1, peers):
+            pltpu.make_async_remote_copy(
+                src_ref=here, dst_ref=here,
+                send_sem=msend.at[ds - 1], recv_sem=mrecv.at[ds - 1, plane],
+                device_id={"seq": lax.rem(s + ds, peers)}, device_id_type=MESH,
+            ).start()
+
+    def bulk(count, send_end, recv_end, core=0):
+        here = block(core, 0, count * rows)
         return pltpu.make_async_remote_copy(
-            src_ref=here, dst_ref=here, send_sem=climb_sem.at[way, plane],
-            recv_sem=recv_sem.at[label(plane, 0, 0)],
-            device_id={"batch": target}, device_id_type=MESH,
+            src_ref=here, dst_ref=here, send_sem=send_end, recv_sem=recv_end,
+            device_id={"batch": lax.rem(me + 1, X * Y * Z)}, device_id_type=MESH,
         )
 
-    def arrival(plane, db, dc):
-        here = block(s, chip_at(s, plane, db, dc))
-        index = label(plane, db, dc)
-        other = lax.rem(me + 1, X * Y * Z)
-        return pltpu.make_async_remote_copy(
-            src_ref=here, dst_ref=here, send_sem=send_sem.at[index], recv_sem=recv_sem.at[index],
-            device_id={"batch": other}, device_id_type=MESH,
-        )
-
-    def mirror(plane, db, dc, ds, core):
-        here = block(core, chip_at(core, plane, db, dc))
-        index = label(plane, db, dc)
-        return pltpu.make_async_remote_copy(
-            src_ref=here, dst_ref=here,
-            send_sem=msend.at[ds - 1, index], recv_sem=mrecv.at[ds - 1, index],
-            device_id={"seq": lax.rem(s + ds, peers)}, device_id_type=MESH,
-        )
-
-    def share(plane, db, dc):
-        for ds in range(1, peers):
-            mirror(plane, db, dc, ds, s).start()
-
-    def forward_plane(plane):
-        for db in range(1, nb):
-            relay((plane, 0, 0), (db, 0)).start()
-        for dc in range(1, nc):
-            relay((plane, 0, 0), (0, dc)).start()
-
-    def middle(g):
-        @pl.when(g < Z)
-        def _():
-            plane = plane_at(g)
-            for db in range(1, nb):
-                arrival(plane, db, 0).wait_recv()
-                for dc in range(1, nc):
-                    relay((plane, db, 0), (0, dc)).start()
-                share(plane, db, 0)
-
-    def enter(g):
-        @pl.when(g < Z)
-        def _():
-            plane = plane_at(g)
-            arrival(plane, 0, 0).wait_recv()
-
-            @pl.when(jnp.logical_and(plane < a, a < Z - 1))
+    def inside(plane):
+        return jnp.logical_and(plane >= 0, plane < Z)
+
+    def needs(distance, side):
+        return jnp.logical_and(has[side], distance + 1 > reach_by[side])
+
+    def stage(d, piece):
+        e = d - 2
+        for side in (-1, 1):
+            plane = a + side * d
+
+            @pl.when(inside(plane))
             def _():
-                climb(plane, 1).start()
-
-            @pl.when(jnp.logical_and(plane > a, a > 0))
+                wait_piece(plane, 0, 0, piece)
+                pl.when(has[-side])(lambda: climb(plane, -side, piece))
+                sideways(plane, piece)
+                share(plane, 0, 0, piece)
+
+            beside = a + side * (d - 1)
+            on = jnp.logical_and(inside(beside), d - 1 <= reach)
+            if side == 1:
+                on = jnp.logical_and(on, d > 1)
+
+            @pl.when(on)
             def _():
-                climb(plane, 0).start()
-
-            forward_plane(plane)
-            share(plane, 0, 0)
-
-    def tail(g):
-        @pl.when(g < Z)
-        def _():
-            plane = plane_at(g)
-            for dc in range(1, nc):
-                for db in range(nb):
-                    arrival(plane, db, dc).wait_recv()
-                    share(plane, db, dc)
+                for db, _ in sides:
+                    wait_piece(beside, db, 0, piece)
+                    for _, dc in fronts:
+                        send(
+                            (beside, db, 0), (beside, db, dc), relay_sem.at[beside],
+                            chip_at(s, a, 0, -dc), piece,
+                        ).start()
+                    share(beside, db, 0, piece)
+
+            if corners:
+                far = a + side * e
+                on = jnp.logical_or(e > reach, needs(e, -side))
+                if side == 1:
+                    on = jnp.logical_and(on, e > 0)
+                else:
+                    on = jnp.logical_or(on, e == 0)
+                on = jnp.logical_and(on, jnp.logical_and(inside(far), e >= 0))
+
+                @pl.when(on)
+                def _():
+                    for corner in corners:
+                        wait_piece(far, *corner, piece)
+                    pl.when(needs(e, -side))(lambda: climb_corners(far, -side, piece))
+                    if side == -1:
+                        pl.when(jnp.logical_and(e == 0, needs(e, side)))(lambda: climb_corners(far, side, piece))
+                    for corner in corners:
+                        share(far, *corner, piece)
+
+    def stage_all(d, lo=0, hi=pieces):
+        def one(piece, _):
+            stage(d, piece)
+            return 0
+
+        lax.fori_loop(lo, hi, one, 0)
+
+    def front_all(d):
+        def one(piece, _):
+            for side in (-1, 1):
+                plane = a + side * d
+                pl.when(inside(plane))(lambda: forwards(plane, piece))
+            return 0
+
+        lax.fori_loop(0, pieces, one, 0)
+
+    def finish(g, lo=0, hi=pieces):
+        plane = plane_at(g)
+        distance = jnp.abs(plane - a)
+        side = jnp.where(plane < a, -1, 1)
+        onward = jnp.where(side < 0, needs(distance, 1), needs(distance, -1))
+
+        def one(piece, _):
+            @pl.when(distance > reach)
+            def _():
+                for db, _ in sides:
+                    wait_piece(plane, db, 0, piece)
+                    share(plane, db, 0, piece)
+
+            for _, dc in fronts:
+                wait_piece(plane, 0, dc, piece)
+                share(plane, 0, dc, piece)
+
+            if corners:
+                late = jnp.logical_and(distance <= reach, jnp.logical_not(onward))
+
+                @pl.when(jnp.logical_and(late, distance > 0))
+                def _():
+                    for corner in corners:
+                        wait_piece(plane, *corner, piece)
+                        share(plane, *corner, piece)
+            return 0
+
+        lax.fori_loop(lo, hi, one, 0)
 
     def mirrored(g):
         plane = plane_at(g)
         for ds in range(1, peers):
             core = lax.rem(s - ds + peers, peers)
-            for db in range(nb):
-                for dc in range(nc):
-                    def wait():
-                        mirror(plane, db, dc, ds, core).wait_recv()
-                    if db or dc:
-                        wait()
-                    else:
-                        pl.when(g > 0)(wait)
+
+            def wait(count):
+                if count:
+                    bulk(count, msend.at[ds - 1], mrecv.at[ds - 1, plane], core).wait_recv()
+
+            if isinstance(g, int):
+                wait(X * Y - 1 if g == 0 else X * Y)
+            else:
+                wait(X * Y)
 
     loads = [
         pltpu.make_async_copy(
@@ -227,15 +322,14 @@
 
     loads[0].wait()
 
-    @pl.when(a < Z - 1)
-    def _():
-        climb(a, 1).start()
-
-    @pl.when(a > 0)
-    def _():
-        climb(a, 0).start()
-
-    forward_plane(a)
+    def own(piece, _):
+        for side in (-1, 1):
+            pl.when(has[side])(lambda: climb(a, side, piece))
+        sideways(a, piece)
+        forwards(a, piece)
+        return 0
+
+    lax.fori_loop(0, pieces, own, 0)
 
     def next_core():
         return {"seq": lax.rem(s + 1, peers)}
@@ -277,23 +371,19 @@
     seg_wide = jnp.broadcast_to(seg_row, (128, length)).T
 
     def first():
-        middle(0)
-        enter(1)
+        stage_all(1, 0, pieces // 2)
 
     def second():
-        enter(2)
-        middle(1)
-
-    def third():
-        enter(3)
-        tail(0)
-
-    events = [first, second, third]
-    early = min(len(events), heads - 1)
+        stage_all(1, pieces // 2, pieces)
+        front_all(1)
+
+    events = [first, second]
+    turns = [1, 2]
+    early = min(len(events), max(heads - 2, 0))
 
     def head(h, _):
         turn = h - jnp.where(s == 0, 1, 0)
-        for number, event in enumerate(events[:early]):
+        for number, event in zip(turns[:early], events):
             pl.when(turn == number)(event)
 
         exponent = jnp.full((1, key_width), exps_ref[h], jnp.int32).astype(jnp.float32)
@@ -349,38 +439,57 @@
     def plane_start(g):
         return pl.multiple_of(plane_at(g) * plane_rows, plane_rows)
 
-    def project(g):
+    def project(g, first=False, last=False):
         start = plane_start(g)
         left = hidden[:, pl.ds(start, plane_rows)]
         for tile in range(columns // TILE):
             cols = pl.ds(tile * TILE, TILE)
             product = mm(left, w_ref[pl.ds(start, plane_rows), cols])
-
-            @pl.when(g == 0)
-            def _():
+            if not first:
+                product = acc[:, cols] + product
+            if last:
+                out_ref[:, cols] = product.astype(jnp.bfloat16)
+            else:
                 acc[:, cols] = product
 
-            @pl.when(g > 0)
-            def _():
-                acc[:, cols] += product
-
-    def step(g, _):
-        middle(g + 2)
-        enter(g + 4)
+    def ready(g):
+        finish(g)
         mirrored(g)
+
+    stage_all(2)
+    front_all(2)
+    if Z > 1:
+        ready(0)
+        project(0, first=True)
+
+    def later(d, _):
+        stage_all(d)
+        front_all(d)
+        return 0
+
+    def middle(g, _):
+        ready(g)
         project(g)
-        tail(g + 1)
         return 0
 
-    lax.fori_loop(0, Z - 1, step, 0)
-    mirrored(Z - 1)
-    start = plane_start(Z - 1)
-    left = hidden[:, pl.ds(start, plane_rows)]
-    for tile in range(columns // TILE):
-        cols = pl.ds(tile * TILE, TILE)
-        product = mm(left, w_ref[pl.ds(start, plane_rows), cols])
-        total = acc[:, cols] + product if Z > 1 else product
-        out_ref[:, cols] = total.astype(jnp.bfloat16)
+    lax.fori_loop(3, Z + 1, later, 0)
+    lax.fori_loop(1, Z - 2, middle, 0)
+    half = pieces // 2
+    if Z > 1:
+        stage_all(Z + 1, 0, half)
+        if Z > 2:
+            ready(Z - 2)
+            project(Z - 2)
+        finish(Z - 1, 0, half)
+
+        def closing(piece, _):
+            stage(Z + 1, piece)
+            finish(Z - 1, piece, piece + 1)
+            return 0
+
+        lax.fori_loop(half, pieces, closing, 0)
+    else:
+        finish(0)
 
     @pl.when(s < peers - 1)
     def _():
@@ -392,32 +501,38 @@
 
         lax.fori_loop(0, heads, sent, 0)
 
+    if sides:
+        bulk(Z * len(sides), side_sem.at[0], recv_sem.at[0]).wait_send()
+    if fronts:
+        bulk(Z * len(fronts), side_sem.at[1], recv_sem.at[0]).wait_send()
+
     def sent_plane(plane, _):
-        for db in range(nb):
-            for dc in range(nc):
-                if db or dc:
-                    arrival(plane, db, dc).wait_send()
-
-                def wait():
-                    for ds in range(1, peers):
-                        mirror(plane, db, dc, ds, s).wait_send()
-
-                if db or dc:
-                    wait()
-                else:
-                    pl.when(plane != a)(wait)
-
-        @pl.when(jnp.logical_and(plane <= a, a < Z - 1))
-        def _():
-            climb(plane, 1).wait_send()
-
-        @pl.when(jnp.logical_and(plane >= a, a > 0))
-        def _():
-            climb(plane, 0).wait_send()
+        if corners:
+            @pl.when(jnp.abs(plane - a) <= reach)
+            def _():
+                bulk(len(corners), relay_sem.at[plane], recv_sem.at[0]).wait_send()
+
+        for side in (-1, 1):
+            away = (a - plane) * side
+            on = jnp.logical_and(has[side], away >= 0)
+
+            @pl.when(on)
+            def _():
+                bulk(1, climb_sem.at[(side + 1) // 2, plane], recv_sem.at[0]).wait_send()
+
+            if corners:
+                @pl.when(jnp.logical_and(on, away + 1 > reach_by[side]))
+                def _():
+                    bulk(len(corners), corner_sem.at[(side + 1) // 2, plane], recv_sem.at[0]).wait_send()
 
         return 0
 
     lax.fori_loop(0, Z, sent_plane, 0)
+    mirrored(Z - 1)
+    project(Z - 1, first=Z == 1, last=True)
+    if X * Y * Z > 1:
+        for ds in range(1, peers):
+            bulk(X * Y * Z - 1, msend.at[ds - 1], recv_sem.at[0]).wait_send()
 
 
 def local(grid, peers, queries, keys, values, gate_rate, segment_ids, decay_exps, out_weight):
@@ -427,11 +542,13 @@
     columns = out_weight.shape[1]
     chips = grid[0] * grid[1] * grid[2]
     chunk = min(CHUNK, length)
+    rows = out_weight.shape[0]
+    pieces = PIECES if rows % (PIECES * 16) == 0 else 1
     kw, vw = key_features // heads, features // heads
     bf16, f32 = jnp.bfloat16, jnp.float32
     anywhere = pl.BlockSpec(memory_space=pl.ANY)
     call = pl.pallas_call(
-        functools.partial(kernel, grid, peers, heads, chunk),
+        functools.partial(kernel, grid, peers, heads, chunk, pieces),
         out_shape=pltpu.VMEM((length, columns), bf16),
         in_specs=[anywhere] * 4
         + [pl.BlockSpec(memory_space=pltpu.VMEM), pl.BlockSpec(memory_space=pltpu.SMEM), anywhere],
@@ -451,11 +568,13 @@
             pltpu.SemaphoreType.DMA((2,)),
             pltpu.SemaphoreType.DMA((heads,)),
             pltpu.SemaphoreType.DMA((heads,)),
-            pltpu.SemaphoreType.DMA((chips,)),
-            pltpu.SemaphoreType.DMA((chips,)),
+            pltpu.SemaphoreType.DMA((2,)),
+            pltpu.SemaphoreType.DMA((grid[0],)),
             pltpu.SemaphoreType.DMA((2, grid[0])),
-            pltpu.SemaphoreType.DMA((max(peers - 1, 1), chips)),
-            pltpu.SemaphoreType.DMA((max(peers - 1, 1), chips)),
+            pltpu.SemaphoreType.DMA((2, grid[0])),
+            pltpu.SemaphoreType.DMA((chips * pieces,)),
+            pltpu.SemaphoreType.DMA((max(peers - 1, 1),)),
+            pltpu.SemaphoreType.DMA((max(peers - 1, 1), grid[0])),
         ],
         compiler_params=pltpu.CompilerParams(
             collective_id=0, has_side_effects=True, vmem_limit_bytes=61 * 1024 * 1024

time: 48.2 us -> 42.3 us (0.88)
  Pallas kernels: 46.7 us -> 40.6 us
    pallas_call x1, Pallas kernels: 46.7 us -> 40.6 us  [local(): call(queries[n], keys[n], values[n], gate_rate[n], segment_ids[n:n + 1],...]
where the time goes in v1:
time: 42.3 us; the launch traced here: 42 us
  Pallas kernels  40.6 us (96%)
  local copies, waits for them, and re-layouts  1.32 us (3%)
    pallas_call x1, Pallas kernels, local(): call(queries[n], keys[n], values[n], gate_rate[n], segment_ids[n:n + 1],...  40.6 us
    unnamed x1, local copies, waits for them, and re-layouts  1.32 us

profile of v1, /device:TPU:0, one launch (start us, length us, event | category | flops | bytes accessed | tf_op | source)
XLA Modules:
  0.0 42.0 jit_solution(4308906488878899947)
XLA Ops:
  0.0 40.6 %gla_project.1 = bf16[512,2048]{1,0:T(8,128)(2,1)S(1)} custom-call(bf16[512,1024]{1,0:T(8,128)(2,1)} %bitcast.7, bf16[512,1024]{1,0:T(8,128)(2,1)} %bitcast.8, bf16[512,2048]{1,0:T(8,128)(2,1)} %bitcast.6, bf16[512,1024]{1,0:T(8,128)(2,1)} %bitcast.9, s32[1,512]{1,0:T(1,128)} %seg_ref.1, s32[4]{0:T(128)} %exps_ref.1, bf16[128,2048]{1,0:T(8,128)(2,1)} %w_hbm.1), custom_call_target="tpu_custom_call" | custom-call | tf_op jit(solution)/shard_map/gla_project/pallas_call | solution.py:585
  40.6 1.3 %copy.9 = bf16[1,512,2048]{2,1,0:T(8,128)(2,1)} copy(bf16[1,512,2048]{2,1,0:T(8,128)(2,1)S(1)} %bitcast.5) | data formatting | bytes 4194304

commit v2 on v1

--- a/solution.py
+++ b/solution.py
@@ -80,9 +80,9 @@
     key_width = keys // heads
     value_width = v_ref.shape[1] // heads
     rows = w_hbm.shape[0]
-    depth = rows // pieces
     columns = w_ref.shape[1]
     part = columns // peers
+    width = part // pieces
     plane_rows = rows * X * Y
     a = me // (X * Y)
     swap = X == Y
@@ -128,14 +128,14 @@
     def label(plane, db, dc):
         return (plane * nb + db) * nc + dc
 
-    def block(core, start, count):
+    def block(core, start, count, piece, pieces_wide=1):
         return w_ref.at[
-            pl.ds(pl.multiple_of(start, depth), count),
-            pl.ds(pl.multiple_of(core * part, part), part),
+            pl.ds(pl.multiple_of(start, rows), count),
+            pl.ds(pl.multiple_of(core * part + piece * width, width), pieces_wide * width),
         ]
 
     def send(held, to, sem, device, piece):
-        here = block(s, chip_at(s, *held) * rows + piece * depth, depth)
+        here = block(s, chip_at(s, *held) * rows, rows, piece)
         return pltpu.make_async_remote_copy(
             src_ref=here, dst_ref=here, send_sem=sem, recv_sem=recv_sem.at[label(*to) * pieces + piece],
             device_id={"batch": device}, device_id_type=MESH,
@@ -163,16 +163,16 @@
         send(to, to, side_sem.at[0], lax.rem(me + 1, X * Y * Z), piece).wait_recv()
 
     def share(plane, db, dc, piece):
-        here = block(s, chip_at(s, plane, db, dc) * rows + piece * depth, depth)
+        here = block(s, chip_at(s, plane, db, dc) * rows, rows, piece)
         for ds in range(1, peers):
             pltpu.make_async_remote_copy(
                 src_ref=here, dst_ref=here,
-                send_sem=msend.at[ds - 1], recv_sem=mrecv.at[ds - 1, plane],
+                send_sem=msend.at[ds - 1], recv_sem=mrecv.at[ds - 1, plane * pieces + piece],
                 device_id={"seq": lax.rem(s + ds, peers)}, device_id_type=MESH,
             ).start()
 
-    def bulk(count, send_end, recv_end, core=0):
-        here = block(core, 0, count * rows)
+    def bulk(count, send_end, recv_end, core=0, piece=0, pieces_wide=pieces):
+        here = block(core, 0, count * rows, piece, pieces_wide)
         return pltpu.make_async_remote_copy(
             src_ref=here, dst_ref=here, send_sem=send_end, recv_sem=recv_end,
             device_id={"batch": lax.rem(me + 1, X * Y * Z)}, device_id_type=MESH,
@@ -185,7 +185,6 @@
         return jnp.logical_and(has[side], distance + 1 > reach_by[side])
 
     def stage(d, piece):
-        e = d - 2
         for side in (-1, 1):
             plane = a + side * d
 
@@ -193,43 +192,53 @@
             def _():
                 wait_piece(plane, 0, 0, piece)
                 pl.when(has[-side])(lambda: climb(plane, -side, piece))
-                sideways(plane, piece)
+                pl.when(d < Z - 1)(lambda: sideways(plane, piece))
                 share(plane, 0, 0, piece)
 
-            beside = a + side * (d - 1)
-            on = jnp.logical_and(inside(beside), d - 1 <= reach)
-            if side == 1:
-                on = jnp.logical_and(on, d > 1)
-
-            @pl.when(on)
+        @pl.when(d == 1)
+        def _():
+            for db, _ in sides:
+                wait_piece(a, db, 0, piece)
+                for _, dc in fronts:
+                    send((a, db, 0), (a, db, dc), relay_sem.at[a], chip_at(s, a, 0, -dc), piece).start()
+                share(a, db, 0, piece)
+
+        if not corners:
+            return
+
+        f = d - 2
+        for side in (-1, 1):
+            plane = a + side * f
+
+            @pl.when(jnp.logical_and(jnp.logical_and(f > 0, f <= reach), inside(plane)))
             def _():
-                for db, _ in sides:
-                    wait_piece(beside, db, 0, piece)
-                    for _, dc in fronts:
+                for _, dc in fronts:
+                    wait_piece(plane, 0, dc, piece)
+                    for db, _ in sides:
                         send(
-                            (beside, db, 0), (beside, db, dc), relay_sem.at[beside],
-                            chip_at(s, a, 0, -dc), piece,
+                            (plane, 0, dc), (plane, db, dc), relay_sem.at[plane],
+                            chip_at(s, a, -db, 0), piece,
                         ).start()
-                    share(beside, db, 0, piece)
-
-            if corners:
-                far = a + side * e
-                on = jnp.logical_or(e > reach, needs(e, -side))
-                if side == 1:
-                    on = jnp.logical_and(on, e > 0)
-                else:
-                    on = jnp.logical_or(on, e == 0)
-                on = jnp.logical_and(on, jnp.logical_and(inside(far), e >= 0))
-
-                @pl.when(on)
-                def _():
-                    for corner in corners:
-                        wait_piece(far, *corner, piece)
-                    pl.when(needs(e, -side))(lambda: climb_corners(far, -side, piece))
-                    if side == -1:
-                        pl.when(jnp.logical_and(e == 0, needs(e, side)))(lambda: climb_corners(far, side, piece))
-                    for corner in corners:
-                        share(far, *corner, piece)
+                    share(plane, 0, dc, piece)
+
+        def corner_step(plane, distance, side, both):
+            for corner in corners:
+                wait_piece(plane, *corner, piece)
+            pl.when(needs(distance, -side))(lambda: climb_corners(plane, -side, piece))
+            if both:
+                pl.when(needs(distance, side))(lambda: climb_corners(plane, side, piece))
+            for corner in corners:
+                share(plane, *corner, piece)
+
+        pl.when(d == 2)(lambda: corner_step(a, 0, -1, True))
+        for side in (-1, 1):
+            late = a + side * (d - 3)
+            on = jnp.logical_and(jnp.logical_and(d > 3, d - 3 <= reach), needs(d - 3, -side))
+            pl.when(jnp.logical_and(on, inside(late)))(lambda: corner_step(late, d - 3, side, False))
+        for side in (-1, 1):
+            far = a + side * f
+            on = jnp.logical_and(jnp.logical_and(f > 0, f > reach), inside(far))
+            pl.when(on)(lambda: corner_step(far, f, side, False))
 
     def stage_all(d, lo=0, hi=pieces):
         def one(piece, _):
@@ -242,30 +251,39 @@
         def one(piece, _):
             for side in (-1, 1):
                 plane = a + side * d
-                pl.when(inside(plane))(lambda: forwards(plane, piece))
+
+                @pl.when(inside(plane))
+                def _():
+                    pl.when(d == Z - 1)(lambda: sideways(plane, piece))
+                    forwards(plane, piece)
             return 0
 
         lax.fori_loop(0, pieces, one, 0)
 
-    def finish(g, lo=0, hi=pieces):
+    def finish(g, lo=0, hi=pieces, beside=True, rest=True, ahead=True):
         plane = plane_at(g)
         distance = jnp.abs(plane - a)
         side = jnp.where(plane < a, -1, 1)
         onward = jnp.where(side < 0, needs(distance, 1), needs(distance, -1))
+        near_by = distance <= reach
 
         def one(piece, _):
-            @pl.when(distance > reach)
-            def _():
+            if beside:
                 for db, _ in sides:
-                    wait_piece(plane, db, 0, piece)
-                    share(plane, db, 0, piece)
-
-            for _, dc in fronts:
-                wait_piece(plane, 0, dc, piece)
-                share(plane, 0, dc, piece)
-
-            if corners:
-                late = jnp.logical_and(distance <= reach, jnp.logical_not(onward))
+                    @pl.when(distance > 0)
+                    def _():
+                        wait_piece(plane, db, 0, piece)
+                        share(plane, db, 0, piece)
+
+            if ahead:
+                for _, dc in fronts:
+                    @pl.when(jnp.logical_or(distance == 0, jnp.logical_not(near_by)) if corners else distance >= 0)
+                    def _():
+                        wait_piece(plane, 0, dc, piece)
+                        share(plane, 0, dc, piece)
+
+            if corners and rest:
+                late = jnp.logical_and(near_by, jnp.logical_not(onward))
 
                 @pl.when(jnp.logical_and(late, distance > 0))
                 def _():
@@ -276,19 +294,15 @@
 
         lax.fori_loop(lo, hi, one, 0)
 
-    def mirrored(g):
+    def mirrored(g, piece):
         plane = plane_at(g)
         for ds in range(1, peers):
             core = lax.rem(s - ds + peers, peers)
-
-            def wait(count):
-                if count:
-                    bulk(count, msend.at[ds - 1], mrecv.at[ds - 1, plane], core).wait_recv()
-
-            if isinstance(g, int):
-                wait(X * Y - 1 if g == 0 else X * Y)
-            else:
-                wait(X * Y)
+            count = X * Y - 1 if isinstance(g, int) and g == 0 else X * Y
+            if count:
+                bulk(
+                    count, msend.at[ds - 1], mrecv.at[ds - 1, plane * pieces + piece], core, piece, 1
+                ).wait_recv()
 
     loads = [
         pltpu.make_async_copy(
@@ -370,21 +384,27 @@
     before = seg_in[...].astype(jnp.float32)[:, length - 1:]
     seg_wide = jnp.broadcast_to(seg_row, (128, length)).T
 
+    quarter = pieces // 4
+
     def first():
-        stage_all(1, 0, pieces // 2)
+        stage_all(1, 0, quarter)
 
     def second():
-        stage_all(1, pieces // 2, pieces)
+        stage_all(1, quarter, pieces - quarter)
+
+    def third():
+        stage_all(1, pieces - quarter, pieces)
         front_all(1)
 
-    events = [first, second]
-    turns = [1, 2]
-    early = min(len(events), max(heads - 2, 0))
+    def fourth():
+        stage_all(2, 0, pieces // 2)
+
+    events = [first, second, third, fourth]
+    lead = jnp.where(s == 0, 2, 0)
 
     def head(h, _):
-        turn = h - jnp.where(s == 0, 1, 0)
-        for number, event in zip(turns[:early], events):
-            pl.when(turn == number)(event)
+        for number, event in enumerate(events):
+            pl.when(h - lead == number)(event)
 
         exponent = jnp.full((1, key_width), exps_ref[h], jnp.int32).astype(jnp.float32)
         scale = jnp.exp2(-exponent) * (-1.0 / 16.0)
@@ -433,34 +453,49 @@
         return 0
 
     lax.fori_loop(0, heads, head, 0)
-    for event in events[early:]:
-        event()
+    for number, event in enumerate(events):
+        pl.when(heads - lead <= number)(event)
 
     def plane_start(g):
         return pl.multiple_of(plane_at(g) * plane_rows, plane_rows)
 
-    def project(g, first=False, last=False):
+    def project(g, first=False):
         start = plane_start(g)
         left = hidden[:, pl.ds(start, plane_rows)]
         for tile in range(columns // TILE):
             cols = pl.ds(tile * TILE, TILE)
             product = mm(left, w_ref[pl.ds(start, plane_rows), cols])
-            if not first:
-                product = acc[:, cols] + product
-            if last:
+            acc[:, cols] = product if first else acc[:, cols] + product
+
+    def ready(g):
+        def one(piece, _):
+            mirrored(g, piece)
+            return 0
+
+        lax.fori_loop(0, pieces, one, 0)
+
+    def settle(lo, hi):
+        start = plane_start(Z - 1)
+
+        def one(piece, _):
+            mirrored(Z - 1, piece)
+            for core in range(peers):
+                cols = pl.ds(pl.multiple_of(core * part + piece * width, width), width)
+                product = mm(hidden[:, pl.ds(start, plane_rows)], w_ref[pl.ds(start, plane_rows), cols])
+                if Z > 1:
+                    product = acc[:, cols] + product
                 out_ref[:, cols] = product.astype(jnp.bfloat16)
-            else:
-                acc[:, cols] = product
-
-    def ready(g):
-        finish(g)
-        mirrored(g)
-
-    stage_all(2)
-    front_all(2)
-    if Z > 1:
-        ready(0)
-        project(0, first=True)
+            return 0
+
+        lax.fori_loop(lo, hi, one, 0)
+
+    def last(lo, hi):
+        def one(piece, _):
+            stage(Z + 1, piece)
+            finish(Z - 1, piece, piece + 1)
+            return 0
+
+        lax.fori_loop(lo, hi, one, 0)
 
     def later(d, _):
         stage_all(d)
@@ -468,28 +503,35 @@
         return 0
 
     def middle(g, _):
+        finish(g, beside=False, ahead=False)
         ready(g)
         project(g)
         return 0
 
-    lax.fori_loop(3, Z + 1, later, 0)
-    lax.fori_loop(1, Z - 2, middle, 0)
-    half = pieces // 2
+    def early(g, _):
+        finish(g, rest=False)
+        return 0
+
+    stage_all(2, pieces // 2, pieces)
+    front_all(2)
     if Z > 1:
-        stage_all(Z + 1, 0, half)
-        if Z > 2:
-            ready(Z - 2)
-            project(Z - 2)
-        finish(Z - 1, 0, half)
-
-        def closing(piece, _):
-            stage(Z + 1, piece)
-            finish(Z - 1, piece, piece + 1)
-            return 0
-
-        lax.fori_loop(half, pieces, closing, 0)
-    else:
         finish(0)
+        ready(0)
+        project(0, first=True)
+    lax.fori_loop(3, Z, later, 0)
+    if Z > 2:
+        lax.fori_loop(1, Z - 2, early, 0)
+        finish(Z - 2, rest=False, ahead=False)
+    if Z > 2:
+        stage_all(Z)
+        finish(Z - 2, beside=False)
+        lax.fori_loop(1, Z - 2, middle, 0)
+    last(0, quarter)
+    if Z > 2:
+        ready(Z - 2)
+        project(Z - 2)
+    last(quarter, pieces - quarter)
+    settle(0, pieces // 2)
 
     @pl.when(s < peers - 1)
     def _():
@@ -528,8 +570,8 @@
         return 0
 
     lax.fori_loop(0, Z, sent_plane, 0)
-    mirrored(Z - 1)
-    project(Z - 1, first=Z == 1, last=True)
+    last(pieces - quarter, pieces)
+    settle(pieces // 2, pieces)
     if X * Y * Z > 1:
         for ds in range(1, peers):
             bulk(X * Y * Z - 1, msend.at[ds - 1], recv_sem.at[0]).wait_send()
@@ -542,13 +584,11 @@
     columns = out_weight.shape[1]
     chips = grid[0] * grid[1] * grid[2]
     chunk = min(CHUNK, length)
-    rows = out_weight.shape[0]
-    pieces = PIECES if rows % (PIECES * 16) == 0 else 1
     kw, vw = key_features // heads, features // heads
     bf16, f32 = jnp.bfloat16, jnp.float32
     anywhere = pl.BlockSpec(memory_space=pl.ANY)
     call = pl.pallas_call(
-        functools.partial(kernel, grid, peers, heads, chunk, pieces),
+        functools.partial(kernel, grid, peers, heads, chunk, PIECES),
         out_shape=pltpu.VMEM((length, columns), bf16),
         in_specs=[anywhere] * 4
         + [pl.BlockSpec(memory_space=pltpu.VMEM), pl.BlockSpec(memory_space=pltpu.SMEM), anywhere],
@@ -572,9 +612,9 @@
             pltpu.SemaphoreType.DMA((grid[0],)),
             pltpu.SemaphoreType.DMA((2, grid[0])),
             pltpu.SemaphoreType.DMA((2, grid[0])),
-            pltpu.SemaphoreType.DMA((chips * pieces,)),
+            pltpu.SemaphoreType.DMA((chips * PIECES,)),
             pltpu.SemaphoreType.DMA((max(peers - 1, 1),)),
-            pltpu.SemaphoreType.DMA((max(peers - 1, 1), grid[0])),
+            pltpu.SemaphoreType.DMA((max(peers - 1, 1), grid[0] * PIECES)),
         ],
         compiler_params=pltpu.CompilerParams(
             collective_id=0, has_side_effects=True, vmem_limit_bytes=61 * 1024 * 1024

time: 42.3 us -> 40.5 us (0.957)
  Pallas kernels: 40.6 us -> 39 us
    pallas_call x1, Pallas kernels: 40.6 us -> 39 us  [local(): call(queries[n], keys[n], values[n], gate_rate[n], segment_ids[n:n + 1],...]
where the time goes in v2:
time: 40.5 us; the launch traced here: 40.3 us
  Pallas kernels  39 us (96%)
  local copies, waits for them, and re-layouts  1.32 us (3%)
    pallas_call x1, Pallas kernels, local(): call(queries[n], keys[n], values[n], gate_rate[n], segment_ids[n:n + 1],...  39 us
    unnamed x1, local copies, waits for them, and re-layouts  1.32 us

profile of v2, /device:TPU:0, one launch (start us, length us, event | category | flops | bytes accessed | tf_op | source)
XLA Modules:
  0.0 40.3 jit_solution(12407521496385648340)
XLA Ops:
  0.0 39.0 %gla_project.1 = bf16[512,2048]{1,0:T(8,128)(2,1)S(1)} custom-call(bf16[512,1024]{1,0:T(8,128)(2,1)} %bitcast.7, bf16[512,1024]{1,0:T(8,128)(2,1)} %bitcast.8, bf16[512,2048]{1,0:T(8,128)(2,1)} %bitcast.6, bf16[512,1024]{1,0:T(8,128)(2,1)} %bitcast.9, s32[1,512]{1,0:T(1,128)} %seg_ref.1, s32[4]{0:T(128)} %exps_ref.1, bf16[128,2048]{1,0:T(8,128)(2,1)} %w_hbm.1), custom_call_target="tpu_custom_call" | custom-call | tf_op jit(solution)/shard_map/gla_project/pallas_call | solution.py:625
  39.0 1.3 %copy.9 = bf16[1,512,2048]{2,1,0:T(8,128)(2,1)} copy(bf16[1,512,2048]{2,1,0:T(8,128)(2,1)S(1)} %bitcast.5) | data formatting | bytes 4194304

commit v3 on v2

--- a/solution.py
+++ b/solution.py
@@ -459,79 +459,92 @@
     def plane_start(g):
         return pl.multiple_of(plane_at(g) * plane_rows, plane_rows)
 
-    def project(g, first=False):
+    def add(g, cols, first, final):
         start = plane_start(g)
-        left = hidden[:, pl.ds(start, plane_rows)]
+        product = mm(hidden[:, pl.ds(start, plane_rows)], w_ref[pl.ds(start, plane_rows), cols])
+        if not first:
+            product = acc[:, cols] + product
+        if final:
+            out_ref[:, cols] = product.astype(jnp.bfloat16)
+        else:
+            acc[:, cols] = product
+
+    def project(g):
         for tile in range(columns // TILE):
-            cols = pl.ds(tile * TILE, TILE)
-            product = mm(left, w_ref[pl.ds(start, plane_rows), cols])
-            acc[:, cols] = product if first else acc[:, cols] + product
-
-    def ready(g):
-        def one(piece, _):
-            mirrored(g, piece)
+            add(g, pl.ds(tile * TILE, TILE), False, False)
+
+    def settle(g, piece, final=False):
+        mirrored(g, piece)
+        for core in range(peers):
+            cols = pl.ds(pl.multiple_of(core * part + piece * width, width), width)
+            add(g, cols, isinstance(g, int) and g == 0, final)
+
+    def loop(lo, hi, body):
+        def one(index, _):
+            body(index)
             return 0
 
-        lax.fori_loop(0, pieces, one, 0)
-
-    def settle(lo, hi):
-        start = plane_start(Z - 1)
-
-        def one(piece, _):
-            mirrored(Z - 1, piece)
-            for core in range(peers):
-                cols = pl.ds(pl.multiple_of(core * part + piece * width, width), width)
-                product = mm(hidden[:, pl.ds(start, plane_rows)], w_ref[pl.ds(start, plane_rows), cols])
-                if Z > 1:
-                    product = acc[:, cols] + product
-                out_ref[:, cols] = product.astype(jnp.bfloat16)
-            return 0
-
         lax.fori_loop(lo, hi, one, 0)
 
-    def last(lo, hi):
-        def one(piece, _):
-            stage(Z + 1, piece)
-            finish(Z - 1, piece, piece + 1)
-            return 0
-
-        lax.fori_loop(lo, hi, one, 0)
-
-    def later(d, _):
+    def later(d):
         stage_all(d)
         front_all(d)
-        return 0
-
-    def middle(g, _):
+
+    def middle(g):
         finish(g, beside=False, ahead=False)
-        ready(g)
+        loop(0, pieces, lambda piece: mirrored(g, piece))
         project(g)
-        return 0
-
-    def early(g, _):
-        finish(g, rest=False)
-        return 0
+
+    def opening(piece):
+        stage(3, piece)
+        settle(0, piece)
+
+    def tidy(piece):
+        finish(Z - 2, piece, piece + 1, beside=False)
+        if Z > 3:
+            finish(Z - 3, piece, piece + 1, beside=False, ahead=False)
+
+    def streaming(piece):
+        stage(Z, piece)
+
+        @pl.when(piece > 0)
+        def _():
+            tidy(piece - 1)
+
+        @pl.when(piece > 1)
+        def _():
+            stream(piece - 2)
+
+    def stream(piece):
+        for g in range(max(Z - 3, 1), Z - 1):
+            settle(g, piece)
+
+    def closing(piece):
+        stage(Z + 1, piece)
+        finish(Z - 1, piece, piece + 1)
+
+        @pl.when(piece > 0)
+        def _():
+            settle(Z - 1, piece - 1, final=True)
 
     stage_all(2, pieces // 2, pieces)
     front_all(2)
+    finish(0)
+    if Z > 3:
+        loop(0, pieces, opening)
+        front_all(3)
+        loop(4, Z, later)
+    elif Z > 1:
+        loop(0, pieces, lambda piece: settle(0, piece))
+    if Z > 2:
+        loop(1, Z - 2, lambda g: finish(g, rest=False))
+        finish(Z - 2, rest=False, ahead=False)
+        loop(1, Z - 3, middle)
+        loop(0, pieces, streaming)
+        tidy(pieces - 1)
+        loop(max(pieces - 2, 0), pieces, stream)
     if Z > 1:
-        finish(0)
-        ready(0)
-        project(0, first=True)
-    lax.fori_loop(3, Z, later, 0)
-    if Z > 2:
-        lax.fori_loop(1, Z - 2, early, 0)
-        finish(Z - 2, rest=False, ahead=False)
-    if Z > 2:
-        stage_all(Z)
-        finish(Z - 2, beside=False)
-        lax.fori_loop(1, Z - 2, middle, 0)
-    last(0, quarter)
-    if Z > 2:
-        ready(Z - 2)
-        project(Z - 2)
-    last(quarter, pieces - quarter)
-    settle(0, pieces // 2)
+        loop(0, pieces, closing)
 
     @pl.when(s < peers - 1)
     def _():
@@ -570,8 +583,10 @@
         return 0
 
     lax.fori_loop(0, Z, sent_plane, 0)
-    last(pieces - quarter, pieces)
-    settle(pieces // 2, pieces)
+    if Z > 1:
+        settle(Z - 1, pieces - 1, final=True)
+    else:
+        loop(0, pieces, lambda piece: settle(0, piece, final=True))
     if X * Y * Z > 1:
         for ds in range(1, peers):
             bulk(X * Y * Z - 1, msend.at[ds - 1], recv_sem.at[0]).wait_send()

time: 40.5 us -> 39.7 us (0.980)
  Pallas kernels: 39 us -> 38.2 us
    pallas_call x1, Pallas kernels: 39 us -> 38.2 us  [local(): call(queries[n], keys[n], values[n], gate_rate[n], segment_ids[n:n + 1],...]
where the time goes in v3:
time: 39.7 us; the launch traced here: 39.6 us
  Pallas kernels  38.2 us (96%)
  local copies, waits for them, and re-layouts  1.32 us (3%)
    pallas_call x1, Pallas kernels, local(): call(queries[n], keys[n], values[n], gate_rate[n], segment_ids[n:n + 1],...  38.2 us
    unnamed x1, local copies, waits for them, and re-layouts  1.32 us

profile of v3, /device:TPU:0, one launch (start us, length us, event | category | flops | bytes accessed | tf_op | source)
XLA Modules:
  0.0 39.6 jit_solution(9399244559339662240)
XLA Ops:
  0.0 38.2 %gla_project.1 = bf16[512,2048]{1,0:T(8,128)(2,1)S(1)} custom-call(bf16[512,1024]{1,0:T(8,128)(2,1)} %bitcast.7, bf16[512,1024]{1,0:T(8,128)(2,1)} %bitcast.8, bf16[512,2048]{1,0:T(8,128)(2,1)} %bitcast.6, bf16[512,1024]{1,0:T(8,128)(2,1)} %bitcast.9, s32[1,512]{1,0:T(1,128)} %seg_ref.1, s32[4]{0:T(128)} %exps_ref.1, bf16[128,2048]{1,0:T(8,128)(2,1)} %w_hbm.1), custom_call_target="tpu_custom_call" | custom-call | tf_op jit(solution)/shard_map/gla_project/pallas_call | solution.py:640
  38.2 1.3 %copy.9 = bf16[1,512,2048]{2,1,0:T(8,128)(2,1)} copy(bf16[1,512,2048]{2,1,0:T(8,128)(2,1)S(1)} %bitcast.5) | data formatting | bytes 4194304

commit v4 on v3

--- a/solution.py
+++ b/solution.py
@@ -12,6 +12,8 @@
 CHUNK = 256
 TILE = 512
 PIECES = 4
+OPENING = [(1, (0, 1)), (2, (1, 4)), (3, (4, 5))]
+CLOSING = [(0, (5, 6)), (1, (6, 7)), (2, (7, 8))]
 
 
 def chip_grid(mesh):
@@ -70,7 +72,7 @@
     grid, peers, heads, chunk, pieces,
     q_hbm, k_hbm, v_hbm, g_hbm, seg_ref, exps_ref, w_hbm,
     out_ref,
-    q_ref, k_ref, v_ref, g_ref, w_ref, hidden, acc, seg_in, state_in, state_out,
+    q_ref, k_ref, v_ref, g_ref, w_ref, hidden, acc, mixed, seg_in, state_in, state_out,
     load_sem, seg_sem, state_send, state_recv, side_sem, relay_sem, climb_sem, corner_sem, recv_sem, msend, mrecv,
 ):
     Z, Y, X = grid
@@ -366,7 +368,6 @@
 
     @pl.when(s == 0)
     def _():
-        state_in[...] = jnp.zeros_like(state_in)
         seg_in[...] = jnp.full(seg_in.shape, -1, jnp.int32)
 
     for load in loads[1:]:
@@ -384,39 +385,33 @@
     before = seg_in[...].astype(jnp.float32)[:, length - 1:]
     seg_wide = jnp.broadcast_to(seg_row, (128, length)).T
 
-    quarter = pieces // 4
-
-    def first():
-        stage_all(1, 0, quarter)
-
-    def second():
-        stage_all(1, quarter, pieces - quarter)
-
-    def third():
-        stage_all(1, pieces - quarter, pieces)
-        front_all(1)
-
-    def fourth():
-        stage_all(2, 0, pieces // 2)
-
-    events = [first, second, third, fourth]
-    lead = jnp.where(s == 0, 2, 0)
+    def relay_steps(lo, hi):
+        def one(number, _):
+            stage(1 + number // pieces, lax.rem(number, pieces))
+            pl.when(number == pieces - 1)(lambda: front_all(1))
+            return 0
+
+        lax.fori_loop(lo, hi, one, 0)
+
+    def relays_at(h, plan):
+        lo = hi = 0
+        for at, (start, stop) in plan:
+            lo, hi = jnp.where(h == at, start, lo), jnp.where(h == at, stop, hi)
+        relay_steps(lo, hi)
+
+    planned = heads == 4 and pieces == 4
+
+    def columns_of(h):
+        key_cols = pl.ds(pl.multiple_of(h * key_width, key_width), key_width)
+        return key_cols, pl.ds(pl.multiple_of(h * value_width, value_width), value_width)
 
     def head(h, _):
-        for number, event in enumerate(events):
-            pl.when(h - lead == number)(event)
+        relays_at(h, OPENING if planned else [])
 
         exponent = jnp.full((1, key_width), exps_ref[h], jnp.int32).astype(jnp.float32)
         scale = jnp.exp2(-exponent) * (-1.0 / 16.0)
-
-        @pl.when(s > 0)
-        def _():
-            state_copy(h).wait_recv()
-
-        state = state_in[h]
-        previous = before
-        key_cols = pl.ds(pl.multiple_of(h * key_width, key_width), key_width)
-        value_cols = pl.ds(pl.multiple_of(h * value_width, value_width), value_width)
+        key_cols, value_cols = columns_of(h)
+        state = previous = offset = None
         for i in range(length // chunk):
             now = pl.ds(i * chunk, chunk)
             log = mm(triangle, g_ref[now, key_cols]) * scale
@@ -431,30 +426,71 @@
             scores = mm_t(q_hi, k_hi) + mm_t(q_hi, k_lo) + mm_t(q_lo, k_hi)
             scores = jnp.where(jnp.logical_and(causal, column == row), scores, 0.0)
             p_hi, p_lo = split(scores)
-            s_hi, s_lo = split(state)
-            carried = mm_t(q_hi, s_hi) + mm_t(q_hi, s_lo) + mm_t(q_lo, s_hi)
-            mixed = mm(p_hi, value) + mm(p_lo, value)
-            mixed = mixed + jnp.where(column == previous, carried, 0.0)
-            power = jnp.mean(mixed * mixed, axis=-1, keepdims=True)
-            hidden[now, value_cols] = (mixed * lax.rsqrt(power + 1.0)).astype(jnp.bfloat16)
+            inner = mm(p_hi, value) + mm(p_lo, value)
+            if i > 0:
+                s_hi, s_lo = split(state)
+                carried = mm_t(q_hi, s_hi) + mm_t(q_hi, s_lo) + mm_t(q_lo, s_hi)
+                inner = inner + jnp.where(column == previous, carried, 0.0)
+            mixed[now, value_cols] = inner
+            if peers > 1:
+                whole = raised_q if i == 0 else raised_q * jnp.exp(offset)
+                q_ref[now, key_cols], g_ref[now, key_cols] = split(whole)
             final = fall[chunk - 1:, :]
+            end = log[chunk - 1:, :]
+            offset = end if i == 0 else offset + end
             last = row[:, chunk - 1:]
             weighted = jnp.where(column == last, raised_k * final, 0.0)
             w_hi, w_lo = split(weighted)
-            kept = jnp.where(last == previous, state * final, 0.0)
-            state = kept + t_mm(value, w_hi) + t_mm(value, w_lo)
+            grown = t_mm(value, w_hi) + t_mm(value, w_lo)
+            state = grown if i == 0 else grown + jnp.where(last == previous, state * final, 0.0)
             previous = last
 
-        @pl.when(s < peers - 1)
-        def _():
-            state_out[h] = state
-            state_copy(h).start()
+        if peers > 1:
+            @pl.when(s == 0)
+            def _():
+                state_out[h] = state
+                state_copy(h).start()
+
+        if peers > 2:
+            @pl.when(jnp.logical_and(s > 0, s < peers - 1))
+            def _():
+                state_copy(h).wait_recv()
+                state_out[h] = state + jnp.where(previous == before, state_in[h] * jnp.exp(offset), 0.0)
+                state_copy(h).start()
 
         return 0
 
+    def close(h, carry):
+        key_cols, value_cols = columns_of(h)
+        if carry:
+            if peers > 2:
+                pl.when(s == peers - 1)(lambda: state_copy(h).wait_recv())
+            else:
+                state_copy(h).wait_recv()
+            s_hi, s_lo = split(state_in[h])
+        for i in range(length // chunk):
+            now = pl.ds(i * chunk, chunk)
+            total = mixed[now, value_cols]
+            if carry:
+                q_hi, q_lo = q_ref[now, key_cols], g_ref[now, key_cols]
+                carried = mm_t(q_hi, s_hi) + mm_t(q_hi, s_lo) + mm_t(q_lo, s_hi)
+                column = seg_wide[i * chunk:(i + 1) * chunk, :1]
+                total = total + jnp.where(column == before, carried, 0.0)
+            power = jnp.mean(total * total, axis=-1, keepdims=True)
+            hidden[now, value_cols] = (total * lax.rsqrt(power + 1.0)).astype(jnp.bfloat16)
+
     lax.fori_loop(0, heads, head, 0)
-    for number, event in enumerate(events):
-        pl.when(heads - lead <= number)(event)
+
+    def close_step(h, _):
+        if peers > 1:
+            pl.when(s > 0)(lambda: close(h, True))
+            pl.when(s == 0)(lambda: close(h, False))
+        else:
+            close(h, False)
+        relays_at(h, CLOSING if planned else [])
+        return 0
+
+    lax.fori_loop(0, heads, close_step, 0)
 
     def plane_start(g):
         return pl.multiple_of(plane_at(g) * plane_rows, plane_rows)
@@ -527,7 +563,7 @@
         def _():
             settle(Z - 1, piece - 1, final=True)
 
-    stage_all(2, pieces // 2, pieces)
+    relay_steps(CLOSING[-1][1][1] if planned else 0, 2 * pieces)
     front_all(2)
     finish(0)
     if Z > 3:
@@ -616,6 +652,7 @@
             pltpu.VMEM((features, columns), bf16),
             pltpu.VMEM((length, features), bf16),
             pltpu.VMEM((length, columns), f32),
+            pltpu.VMEM((length, features), f32),
             pltpu.VMEM((1, length), jnp.int32),
             pltpu.VMEM((heads, vw, kw), f32),
             pltpu.VMEM((heads, vw, kw), f32),

time: 39.7 us -> 38.8 us (0.977)
  Pallas kernels: 38.2 us -> 37.3 us
    pallas_call x1, Pallas kernels: 38.2 us -> 37.3 us  [local(): call(queries[n], keys[n], values[n], gate_rate[n], segment_ids[n:n + 1],...]
where the time goes in v4:
time: 38.8 us; the launch traced here: 38.6 us
  Pallas kernels  37.3 us (96%)
  local copies, waits for them, and re-layouts  1.32 us (3%)
    pallas_call x1, Pallas kernels, local(): call(queries[n], keys[n], values[n], gate_rate[n], segment_ids[n:n + 1],...  37.3 us
    unnamed x1, local copies, waits for them, and re-layouts  1.32 us

profile of v4, /device:TPU:0, one launch (start us, length us, event | category | flops | bytes accessed | tf_op | source)
XLA Modules:
  0.0 38.6 jit_solution(828943768767798575)
XLA Ops:
  0.0 37.3 %gla_project.1 = bf16[512,2048]{1,0:T(8,128)(2,1)S(1)} custom-call(bf16[512,1024]{1,0:T(8,128)(2,1)} %bitcast.7, bf16[512,1024]{1,0:T(8,128)(2,1)} %bitcast.8, bf16[512,2048]{1,0:T(8,128)(2,1)} %bitcast.6, bf16[512,1024]{1,0:T(8,128)(2,1)} %bitcast.9, s32[1,512]{1,0:T(1,128)} %seg_ref.1, s32[4]{0:T(128)} %exps_ref.1, bf16[128,2048]{1,0:T(8,128)(2,1)} %w_hbm.1), custom_call_target="tpu_custom_call" | custom-call | tf_op jit(solution)/shard_map/gla_project/pallas_call | solution.py:677
  37.3 1.3 %copy.9 = bf16[1,512,2048]{2,1,0:T(8,128)(2,1)} copy(bf16[1,512,2048]{2,1,0:T(8,128)(2,1)S(1)} %bitcast.5) | data formatting | bytes 4194304

commit v5 on v4

--- a/solution.py
+++ b/solution.py
@@ -12,8 +12,8 @@
 CHUNK = 256
 TILE = 512
 PIECES = 4
-OPENING = [(1, (0, 1)), (2, (1, 4)), (3, (4, 5))]
-CLOSING = [(0, (5, 6)), (1, (6, 7)), (2, (7, 8))]
+OPENING = [(1, (0, 1)), (2, (1, 4)), (3, (4, 6))]
+CLOSING = [(0, (6, 7)), (1, (7, 8))]
 
 
 def chip_grid(mesh):
@@ -73,7 +73,7 @@
     q_hbm, k_hbm, v_hbm, g_hbm, seg_ref, exps_ref, w_hbm,
     out_ref,
     q_ref, k_ref, v_ref, g_ref, w_ref, hidden, acc, mixed, seg_in, state_in, state_out,
-    load_sem, seg_sem, state_send, state_recv, side_sem, relay_sem, climb_sem, corner_sem, recv_sem, msend, mrecv,
+    load_sem, seg_sem, state_send, state_recv, side_sem, relay_sem, climb_sem, corner_sem, recv_sem, msend, mrecv, mwhole,
 ):
     Z, Y, X = grid
     s = lax.axis_index("seq")
@@ -173,6 +173,16 @@
                 device_id={"seq": lax.rem(s + ds, peers)}, device_id_type=MESH,
             ).start()
 
+    def share_whole(plane, db, dc, piece):
+        @pl.when(piece == pieces - 1)
+        def _():
+            here = block(s, chip_at(s, plane, db, dc) * rows, rows, 0, pieces)
+            for ds in range(1, peers):
+                pltpu.make_async_remote_copy(
+                    src_ref=here, dst_ref=here, send_sem=msend.at[ds - 1], recv_sem=mwhole.at[ds - 1, plane],
+                    device_id={"seq": lax.rem(s + ds, peers)}, device_id_type=MESH,
+                ).start()
+
     def bulk(count, send_end, recv_end, core=0, piece=0, pieces_wide=pieces):
         here = block(core, 0, count * rows, piece, pieces_wide)
         return pltpu.make_async_remote_copy(
@@ -195,7 +205,7 @@
                 wait_piece(plane, 0, 0, piece)
                 pl.when(has[-side])(lambda: climb(plane, -side, piece))
                 pl.when(d < Z - 1)(lambda: sideways(plane, piece))
-                share(plane, 0, 0, piece)
+                share_whole(plane, 0, 0, piece)
 
         @pl.when(d == 1)
         def _():
@@ -203,7 +213,7 @@
                 wait_piece(a, db, 0, piece)
                 for _, dc in fronts:
                     send((a, db, 0), (a, db, dc), relay_sem.at[a], chip_at(s, a, 0, -dc), piece).start()
-                share(a, db, 0, piece)
+                share_whole(a, db, 0, piece)
 
         if not corners:
             return
@@ -230,7 +240,7 @@
             if both:
                 pl.when(needs(distance, side))(lambda: climb_corners(plane, side, piece))
             for corner in corners:
-                share(plane, *corner, piece)
+                (share_whole if both else share)(plane, *corner, piece)
 
         pl.when(d == 2)(lambda: corner_step(a, 0, -1, True))
         for side in (-1, 1):
@@ -282,7 +292,7 @@
                     @pl.when(jnp.logical_or(distance == 0, jnp.logical_not(near_by)) if corners else distance >= 0)
                     def _():
                         wait_piece(plane, 0, dc, piece)
-                        share(plane, 0, dc, piece)
+                        (share_whole if isinstance(g, int) and g == 0 else share)(plane, 0, dc, piece)
 
             if corners and rest:
                 late = jnp.logical_and(near_by, jnp.logical_not(onward))
@@ -298,10 +308,16 @@
 
     def mirrored(g, piece):
         plane = plane_at(g)
+        own_plane = isinstance(g, int) and g == 0
         for ds in range(1, peers):
             core = lax.rem(s - ds + peers, peers)
-            count = X * Y - 1 if isinstance(g, int) and g == 0 else X * Y
-            if count:
+            count = X * Y - 1
+
+            @pl.when(piece == 0)
+            def _():
+                bulk(count if own_plane else 1, msend.at[ds - 1], mwhole.at[ds - 1, plane], core).wait_recv()
+
+            if count and not own_plane:
                 bulk(
                     count, msend.at[ds - 1], mrecv.at[ds - 1, plane * pieces + piece], core, piece, 1
                 ).wait_recv()
@@ -667,6 +683,7 @@
             pltpu.SemaphoreType.DMA((chips * PIECES,)),
             pltpu.SemaphoreType.DMA((max(peers - 1, 1),)),
             pltpu.SemaphoreType.DMA((max(peers - 1, 1), grid[0] * PIECES)),
+            pltpu.SemaphoreType.DMA((max(peers - 1, 1), grid[0])),
         ],
         compiler_params=pltpu.CompilerParams(
             collective_id=0, has_side_effects=True, vmem_limit_bytes=61 * 1024 * 1024

time: 38.8 us -> 39.1 us (level)
  no operation moved by 1% of the time
where the time goes in v5:
time: 39.1 us; the launch traced here: 38.9 us
  Pallas kernels  37.6 us (96%)
  local copies, waits for them, and re-layouts  1.32 us (3%)
    pallas_call x1, Pallas kernels, local(): call(queries[n], keys[n], values[n], gate_rate[n], segment_ids[n:n + 1],...  37.6 us
    unnamed x1, local copies, waits for them, and re-layouts  1.32 us

profile of v5, /device:TPU:0, one launch (start us, length us, event | category | flops | bytes accessed | tf_op | source)
XLA Modules:
  0.0 38.9 jit_solution(11702477300778395950)
XLA Ops:
  0.0 37.6 %gla_project.1 = bf16[512,2048]{1,0:T(8,128)(2,1)S(1)} custom-call(bf16[512,1024]{1,0:T(8,128)(2,1)} %bitcast.7, bf16[512,1024]{1,0:T(8,128)(2,1)} %bitcast.8, bf16[512,2048]{1,0:T(8,128)(2,1)} %bitcast.6, bf16[512,1024]{1,0:T(8,128)(2,1)} %bitcast.9, s32[1,512]{1,0:T(1,128)} %seg_ref.1, s32[4]{0:T(128)} %exps_ref.1, bf16[128,2048]{1,0:T(8,128)(2,1)} %w_hbm.1), custom_call_target="tpu_custom_call" | custom-call | tf_op jit(solution)/shard_map/gla_project/pallas_call | solution.py:694
  37.6 1.3 %copy.9 = bf16[1,512,2048]{2,1,0:T(8,128)(2,1)} copy(bf16[1,512,2048]{2,1,0:T(8,128)(2,1)S(1)} %bitcast.5) | data formatting | bytes 4194304
